TPU v7x, 32 devices: a whole 2x2x4 slice. The times are simulated.
32 devices in a mesh: seq: 16 (over z, x, core), head: 2 (over y).
Axes of the slice: x: 2, y: 2, z: 4, core: 2. Of those that a mesh axis runs over, the one named last changes fastest.
Arguments:
- query: bfloat16 [8192, 1024], P('seq', 'head'), may hold values from -6 to 6
- key_rows: bfloat16 [8192, 128], P('seq'), may hold values from -6 to 6
- value_rows: bfloat16 [8192, 128], P('seq'), may hold values from -6 to 6
- output: bfloat16 [8192, 1024], P('seq', 'head'), may hold values from -1.5 to 1.5
- grad_output: bfloat16 [8192, 1024], P('seq', 'head'), may hold values from -144 to 144
- log_norm: float32 [8, 8192], P('head', 'seq'), may hold values from 0.5 to 12
- stripe: int32 [16], replicated, may hold values from 0 to 15, each once
Outputs:
- grad_query: bfloat16 [8192, 1024], P('seq', 'head')
- grad_key: bfloat16 [8192, 128], P(('seq', 'head'))
- grad_value: bfloat16 [8192, 128], P(('seq', 'head'))
Inputs may be any that keep to these rules, and one draw needn't show every extreme that they name: stripe is a permutation of 0 to 15.
All inputs are finite; a program needn't handle non-finite values.
Results may differ from a plain program's by a relative error of at most 0.0051.
Values may be sent and summed in bfloat16 or wider, within the bound.
No kernel may reach another device: no remote copies, remote signals or barrier semaphores. Data moves between devices by JAX's collectives and lax.ppermute only.
A program may use at most 192 MiB of HBM per device.

v0:
```python
import jax
import jax.numpy as jnp
from jax import lax
from jax.sharding import PartitionSpec as P

WINDOW = 8


def from_behind(block, axis, distance):
    devices = range(lax.axis_size(axis))
    route = [((i - distance) % len(devices), i) for i in devices]
    return lax.ppermute(block, axis, route)


def block_terms(query_heads, grad_heads, lse_rows, delta_rows, kv_pair, diag_open):
    key_block = kv_pair[0]
    value_block = kv_pair[1]
    extent = key_block.shape[0]
    factor = key_block.shape[1] ** (-0.5)
    scores = (
        jnp.einsum("shd,td->hst", query_heads, key_block, preferred_element_type=jnp.float32)
        * factor
    )
    row_ids = lax.broadcasted_iota(jnp.int32, (extent, extent), 0)
    col_ids = lax.broadcasted_iota(jnp.int32, (extent, extent), 1)
    allowed = (col_ids < row_ids) | (col_ids == row_ids) & diag_open
    weights = jnp.where(allowed[None], jnp.exp(scores - lse_rows[:, :, None]), 0.0)
    weights_low = weights.astype(jnp.bfloat16)
    grad_values = jnp.einsum(
        "hst,shd->td", weights_low, grad_heads, preferred_element_type=jnp.float32
    )
    grad_weights = jnp.einsum(
        "shd,td->hst", grad_heads, value_block, preferred_element_type=jnp.float32
    )
    grad_scores = (factor * weights * (grad_weights - delta_rows[:, :, None])).astype(jnp.bfloat16)
    grad_query = jnp.einsum(
        "hst,td->shd", grad_scores, key_block, preferred_element_type=jnp.float32
    )
    grad_keys = jnp.einsum(
        "hst,shd->td", grad_scores, query_heads, preferred_element_type=jnp.float32
    )
    return (grad_query, jnp.stack([grad_keys, grad_values]))


def stripe_at(stripe, where_index):
    slot_ids = lax.broadcasted_iota(jnp.int32, stripe.shape, 0)
    return jnp.sum(jnp.where(slot_ids == where_index, stripe, 0))


def shards(query, key_rows, value_rows, output, grad_output, log_norm, stripe):
    extent = query.shape[0]
    head_dim = key_rows.shape[1]
    local_heads = query.shape[1] // head_dim
    query_heads = query.reshape(extent, local_heads, head_dim)
    grad_heads = grad_output.reshape(extent, local_heads, head_dim)
    output_heads = output.reshape(extent, local_heads, head_dim)
    delta_rows = jnp.sum(
        grad_heads.astype(jnp.float32) * output_heads.astype(jnp.float32), axis=2
    ).T
    cycle_length = lax.axis_size("seq")
    cycle_index = lax.axis_index("seq")
    own_stripe = stripe_at(stripe, cycle_index)

    def compute(kv_pair, offset):
        source = (cycle_index - offset) % cycle_length
        diag_open = stripe_at(stripe, source) <= own_stripe
        query_part, key_part = block_terms(
            query_heads, grad_heads, log_norm, delta_rows, kv_pair, diag_open
        )
        return (query_part, key_part)

    kv_pair = jnp.stack([key_rows, value_rows])
    grad_query, own_part = compute(kv_pair, 0)
    kv_pair = from_behind(kv_pair, "seq", WINDOW - 1)
    carried = jnp.zeros_like(own_part)
    for offset in range(WINDOW - 1, 0, -1):
        query_part, key_part = compute(kv_pair, offset)
        grad_query = grad_query + query_part
        carried = from_behind(carried + key_part, "seq", -1)
        if offset > 1:
            kv_pair = from_behind(kv_pair, "seq", -1)
    carried = carried + own_part
    summed = lax.psum_scatter(carried, "head", scatter_dimension=1, tiled=True)
    grad_key = summed[0].astype(jnp.bfloat16)
    grad_value = summed[1].astype(jnp.bfloat16)
    return (
        grad_query.reshape(extent, local_heads * head_dim).astype(jnp.bfloat16),
        grad_key,
        grad_value,
    )


def solution(mesh):
    placed = (
        P("seq", "head"),
        P("seq", None),
        P("seq", None),
        P("seq", "head"),
        P("seq", "head"),
        P("head", "seq"),
        P(),
    )
    return jax.shard_map(
        shards,
        mesh=mesh,
        in_specs=placed,
        out_specs=(P("seq", "head"), P(("seq", "head"), None), P(("seq", "head"), None)),
        check_vma=False,
    )
```

profile of v0, /device:TPU:1, one launch (start us, length us, event | category | flops | bytes accessed | tf_op | source)
XLA Modules:
  0.0 165.7 jit_solution(5302465309677904088)
XLA Ops:
  7.2 1.0 pad_maximum_fusion.1
  8.3 3.7 %collective-permute-start = (bf16[2,512,128]{2,1,0:T(8,128)(2,1)S(1)}, bf16[2,512,128]{2,1,0:T(8,128)(2,1)S(1)}, u32[]{:S(2)}, u32[]{:S(2)}) collective-permute-start(bf16[2,512,128]{2,1,0:T(8,128)(2,1)S(1)} %pad_maximum_fusion.1), channel_id=1, source_target_pairs={{18,0},{20,2},{22,4},{24,6},{26,8},{28,10},{30,12},{0,14},{2,16},{... | collective-permute-start | bytes 786440 | tf_op jit(solution)/shard_map/ppermute | solution.py:12
  12.0 1.5 fusion.163
  14.8 0.8 fusion.110
  15.6 1.4 reshape.77
  17.0 1.2 reshape.76
  18.2 0.6 multiply_reduce_fusion
  28.6 0.7 fusion.150
  29.3 0.9 fusion.72
  30.3 1.6 fusion.29
  31.9 0.5 convolution_bitcast_fusion.7
  32.4 0.7 convolution_bitcast_fusion.8
  33.2 0.7 fusion.148
  33.9 0.9 fusion.75
  34.8 1.7 %fusion.25 = bf16[4,512,512]{1,2,0:T(8,128)(2,1)S(1)} fusion(f32[512,512,4]{1,0,2:T(8,128)S(1)} %fusion.148, f32[4,512]{1,0:T(4,128)S(1)} %copy.61, f32[4,512]{1,0:T(4,128)S(1)} %copy-done.12, pred[512,512]{0,1:T(8,128)(4,1)S(1)} %copy-done.10, bf16[2,512,128]{2,1,0:T(8,128)(2,1)S(1)} %collective-permute-done, bf16[512,512]{1,0:T(8,128)(2,1)S(1)} %copy-done.9), kind=kOutput, calls=%fused_computation.38 | convolution fusion | flops 275775488 | bytes 7225344 | tf_op jit(solution)/shard_map/shd,td->hst/dot_general | solution.py:32
  36.5 0.7 convolution_bitcast_fusion.15
  37.3 2.4 %collective-permute-start.1 = (bf16[2,512,128]{2,1,0:T(8,128)(2,1)S(1)}, bf16[2,512,128]{2,1,0:T(8,128)(2,1)S(1)}, u32[]{:S(2)}, u32[]{:S(2)}) collective-permute-start(bf16[2,512,128]{2,1,0:T(8,128)(2,1)S(1)} %collective-permute-done), channel_id=1, source_target_pairs={{2,0},{4,2},{6,4},{8,6},{10,8},{12,10},{14,12},{16,14},{18,16},{20... | collective-permute-start | bytes 786440 | tf_op jit(solution)/shard_map/ppermute | solution.py:12
  40.2 8.5 %collective-permute-done.1 = bf16[2,512,128]{2,1,0:T(8,128)(2,1)S(1)} collective-permute-done((bf16[2,512,128]{2,1,0:T(8,128)(2,1)S(1)}, bf16[2,512,128]{2,1,0:T(8,128)(2,1)S(1)}, u32[]{:S(2)}, u32[]{:S(2)}) %collective-permute-start.1) | collective-permute-done | bytes 262176 | tf_op jit(solution)/shard_map/ppermute | solution.py:12
  48.7 0.7 fusion.146
  49.4 0.7 collective-permute-start.2
  50.1 1.6 fusion.21
  51.8 0.9 fusion.78
  52.7 0.7 convolution_bitcast_fusion.14
  53.5 4.7 %collective-permute-start.8 = (f32[2,512,128]{2,1,0:T(8,128)S(1)}, f32[2,512,128]{2,1,0:T(8,128)S(1)}, u32[]{:S(2)}, u32[]{:S(2)}) collective-permute-start(f32[2,512,128]{2,1,0:T(8,128)S(1)} %maximum_add_fusion), channel_id=1, source_target_pairs={{2,0},{4,2},{6,4},{8,6},{10,8},{12,10},{14,12},{16,14},{18,16},{20... | collective-permute-start | bytes 1572872 | tf_op jit(solution)/shard_map/ppermute | solution.py:12
  58.2 0.7 fusion.144
  58.9 0.9 fusion.81
  59.9 1.6 fusion.17
  62.0 0.7 convolution_bitcast_fusion.13
  62.7 4.7 %collective-permute-done.3 = bf16[2,512,128]{2,1,0:T(8,128)(2,1)S(1)} collective-permute-done((bf16[2,512,128]{2,1,0:T(8,128)(2,1)S(1)}, bf16[2,512,128]{2,1,0:T(8,128)(2,1)S(1)}, u32[]{:S(2)}, u32[]{:S(2)}) %collective-permute-start.3) | collective-permute-done | bytes 262176 | tf_op jit(solution)/shard_map/ppermute | solution.py:12
  67.4 0.7 fusion.142
  68.1 3.2 %collective-permute-start.4 = (bf16[2,512,128]{2,1,0:T(8,128)(2,1)S(1)}, bf16[2,512,128]{2,1,0:T(8,128)(2,1)S(1)}, u32[]{:S(2)}, u32[]{:S(2)}) collective-permute-start(bf16[2,512,128]{2,1,0:T(8,128)(2,1)S(1)} %collective-permute-done.3), channel_id=1, source_target_pairs={{2,0},{4,2},{6,4},{8,6},{10,8},{12,10},{14,12},{16,14},{18,16},{20... | collective-permute-start | bytes 786440 | tf_op jit(solution)/shard_map/ppermute | solution.py:12
  71.3 1.6 fusion.13
  72.9 0.9 fusion.84
  73.9 0.7 convolution_bitcast_fusion.12
  74.7 4.9 %collective-permute-start.9 = (f32[2,512,128]{2,1,0:T(8,128)S(1)}, f32[2,512,128]{2,1,0:T(8,128)S(1)}, u32[]{:S(2)}, u32[]{:S(2)}) collective-permute-start(f32[2,512,128]{2,1,0:T(8,128)S(1)} %maximum_add_fusion.1), channel_id=1, source_target_pairs={{2,0},{4,2},{6,4},{8,6},{10,8},{12,10},{14,12},{16,14},{18,16},{20... | collective-permute-start | bytes 1572872 | tf_op jit(solution)/shard_map/ppermute | solution.py:12
  79.5 0.7 fusion.140
  80.2 0.9 fusion.87
  81.2 1.6 fusion.9
  83.1 0.7 convolution_bitcast_fusion.11
  83.8 4.9 %collective-permute-done.5 = bf16[2,512,128]{2,1,0:T(8,128)(2,1)S(1)} collective-permute-done((bf16[2,512,128]{2,1,0:T(8,128)(2,1)S(1)}, bf16[2,512,128]{2,1,0:T(8,128)(2,1)S(1)}, u32[]{:S(2)}, u32[]{:S(2)}) %collective-permute-start.5) | collective-permute-done | bytes 262176 | tf_op jit(solution)/shard_map/ppermute | solution.py:12
  88.7 0.7 fusion.138
  89.4 3.0 %collective-permute-start.6 = (bf16[2,512,128]{2,1,0:T(8,128)(2,1)S(1)}, bf16[2,512,128]{2,1,0:T(8,128)(2,1)S(1)}, u32[]{:S(2)}, u32[]{:S(2)}) collective-permute-start(bf16[2,512,128]{2,1,0:T(8,128)(2,1)S(1)} %collective-permute-done.5), channel_id=1, source_target_pairs={{2,0},{4,2},{6,4},{8,6},{10,8},{12,10},{14,12},{16,14},{18,16},{20... | collective-permute-start | bytes 786440 | tf_op jit(solution)/shard_map/ppermute | solution.py:12
  92.4 1.6 fusion.5
  94.1 4.7 %collective-permute-start.10 = (f32[2,512,128]{2,1,0:T(8,128)S(1)}, f32[2,512,128]{2,1,0:T(8,128)S(1)}, u32[]{:S(2)}, u32[]{:S(2)}) collective-permute-start(f32[2,512,128]{2,1,0:T(8,128)S(1)} %maximum_add_fusion.2), channel_id=1, source_target_pairs={{2,0},{4,2},{6,4},{8,6},{10,8},{12,10},{14,12},{16,14},{18,16},{20... | collective-permute-start | bytes 1572872 | tf_op jit(solution)/shard_map/ppermute | solution.py:12
  98.8 0.9 fusion.90
  99.7 0.7 convolution_bitcast_fusion.10
  100.4 2.3 %collective-permute-done.10 = f32[2,512,128]{2,1,0:T(8,128)S(1)} collective-permute-done((f32[2,512,128]{2,1,0:T(8,128)S(1)}, f32[2,512,128]{2,1,0:T(8,128)S(1)}, u32[]{:S(2)}, u32[]{:S(2)}) %collective-permute-start.10) | collective-permute-done | bytes 524320 | tf_op jit(solution)/shard_map/ppermute | solution.py:12
  102.8 3.8 %collective-permute-start.11 = (f32[2,512,128]{2,1,0:T(8,128)S(1)}, f32[2,512,128]{2,1,0:T(8,128)S(1)}, u32[]{:S(2)}, u32[]{:S(2)}) collective-permute-start(f32[2,512,128]{2,1,0:T(8,128)S(1)} %maximum_add_fusion.3), channel_id=1, source_target_pairs={{2,0},{4,2},{6,4},{8,6},{10,8},{12,10},{14,12},{16,14},{18,16},{20... | collective-permute-start | bytes 1572872 | tf_op jit(solution)/shard_map/ppermute | solution.py:12
  106.6 0.7 fusion.136
  107.3 1.7 %fusion.1 = bf16[4,512,512]{1,2,0:T(8,128)(2,1)S(1)} fusion(f32[512,512,4]{1,0,2:T(8,128)S(1)} %fusion.136, f32[4,512]{1,0:T(4,128)S(1)} %copy.61, f32[4,512]{1,0:T(4,128)S(1)} %copy-done.12, pred[512,512]{0,1:T(8,128)(4,1)S(1)} %fusion.104, bf16[2,512,128]{2,1,0:T(8,128)(2,1)S(1)} %collective-permute-done.6, bf16[512,512]{1,0:T(8,128)(2,1)S(1)} %copy-done.9), kind=kOutput, calls=%fused_computation.2 | convolution fusion | flops 275775488 | bytes 7225344 | tf_op jit(solution)/shard_map/shd,td->hst/dot_general | solution.py:32
  109.0 2.5 %collective-permute-done.11 = f32[2,512,128]{2,1,0:T(8,128)S(1)} collective-permute-done((f32[2,512,128]{2,1,0:T(8,128)S(1)}, f32[2,512,128]{2,1,0:T(8,128)S(1)}, u32[]{:S(2)}, u32[]{:S(2)}) %collective-permute-start.11) | collective-permute-done | bytes 524320 | tf_op jit(solution)/shard_map/ppermute | solution.py:12
  111.5 6.5 %collective-permute-start.12 = (f32[2,512,128]{2,1,0:T(8,128)S(1)}, f32[2,512,128]{2,1,0:T(8,128)S(1)}, u32[]{:S(2)}, u32[]{:S(2)}) collective-permute-start(f32[2,512,128]{2,1,0:T(8,128)S(1)} %maximum_add_fusion.4), channel_id=1, source_target_pairs={{2,0},{4,2},{6,4},{8,6},{10,8},{12,10},{14,12},{16,14},{18,16},{20... | collective-permute-start | bytes 1572872 | tf_op jit(solution)/shard_map/ppermute | solution.py:12
  118.0 0.7 convolution_bitcast_fusion.9
  118.7 0.9 fusion.93
  119.7 0.5 collective-permute-done.12
  120.3 9.4 %collective-permute-start.13 = (f32[2,512,128]{2,1,0:T(8,128)S(1)}, f32[2,512,128]{2,1,0:T(8,128)S(1)}, u32[]{:S(2)}, u32[]{:S(2)}) collective-permute-start(f32[2,512,128]{2,1,0:T(8,128)S(1)} %maximum_add_fusion.5), channel_id=1, source_target_pairs={{2,0},{4,2},{6,4},{8,6},{10,8},{12,10},{14,12},{16,14},{18,16},{20... | collective-permute-start | bytes 1572872 | tf_op jit(solution)/shard_map/ppermute | solution.py:12
  130.7 0.6 collective-permute-done.13
  131.2 0.9 maximum_add_fusion.6
  132.2 2.2 %fusion.67 = f32[512,4,128]{0,2,1:T(8,128)S(1)} fusion(f32[512,4,128]{0,2,1:T(8,128)S(1)} %fusion.68, bf16[4,512,512]{1,2,0:T(8,128)(2,1)} %copy-done.1, bf16[2,512,128]{2,1,0:T(8,128)(2,1)S(1)} %collective-permute-done.3), kind=kOutput, calls=%fused_computation.79 | convolution fusion | flops 268697600 | bytes 4325376 | tf_op jit(solution)/shard_map/hst,td->shd/dot_general | solution.py:36
  135.5 0.7 copy-done.7
  136.6 1.0 copy.108
  137.6 19.6 %reduce-scatter.2.cloned.1.call-done = f32[2,256,128]{2,1,0:T(8,128)} async-done(((f32[2,512,128]{2,1,0:T(8,128)}), f32[2,256,128]{2,1,0:T(8,128)}) %reduce-scatter.2.cloned.1.call-update) | async-done | bytes 262160 | tf_op jit(solution)/shard_map/reduce_scatter | solution.py:83
  157.2 1.0 convert.5
  158.2 0.7 slice_bitcast_fusion.35
  (58 shorter events, 5.2 us)
Async XLA Ops:
  7.2 21.4 %copy-start = (bf16[512,512]{1,0:T(8,128)(2,1)S(1)}, bf16[512,512]{1,0:T(8,128)(2,1)}, u32[]{:S(2)}) copy-start(bf16[512,512]{1,0:T(8,128)(2,1)} %param.7) | copy-start | bytes 1572868
  7.2 21.4 %copy-start.8 = (bf16[512,128]{1,0:T(8,128)(2,1)S(1)}, bf16[512,128]{1,0:T(8,128)(2,1)}, u32[]{:S(2)}) copy-start(bf16[512,128]{1,0:T(8,128)(2,1)} %param.8) | copy-start | bytes 393220
  7.2 150.1 %reduce-scatter.2.cloned.1.call-start = ((), (), s32[]{:S(2)}) async-start(), calls=%async_computation.1 | async-start | bytes 786432 | tf_op jit(solution)/shard_map/reduce_scatter | solution.py:83
  8.3 24.9 %collective-permute-start = (bf16[2,512,128]{2,1,0:T(8,128)(2,1)S(1)}, bf16[2,512,128]{2,1,0:T(8,128)(2,1)S(1)}, u32[]{:S(2)}, u32[]{:S(2)}) collective-permute-start(bf16[2,512,128]{2,1,0:T(8,128)(2,1)S(1)} %pad_maximum_fusion.1), channel_id=1, source_target_pairs={{18,0},{20,2},{22,4},{24,6},{26,8},{28,10},{30,12},{0,14},{2,16},{... | collective-permute-start | bytes 786440 | tf_op jit(solution)/shard_map/ppermute | solution.py:12
  18.1 11.2 %copy-start.9 = (bf16[512,512]{1,0:T(8,128)(2,1)S(1)}, bf16[512,512]{1,0:T(8,128)(2,1)}, u32[]{:S(2)}) copy-start(bf16[512,512]{1,0:T(8,128)(2,1)} %param.11) | copy-start | bytes 1572868
  18.1 11.2 %copy-start.12 = (f32[4,512]{1,0:T(4,128)S(1)}, f32[4,512]{1,0:T(4,128)}, u32[]{:S(2)}) copy-start(f32[4,512]{1,0:T(4,128)} %param.12) | copy-start | bytes 24580
  29.3 1.0 copy-start.11
  32.4 1.4 copy-start.10
  37.2 16.2 %collective-permute-start.7 = (f32[2,512,128]{2,1,0:T(8,128)S(1)}, f32[2,512,128]{2,1,0:T(8,128)S(1)}, u32[]{:S(2)}, u32[]{:S(2)}) collective-permute-start(f32[2,512,128]{2,1,0:T(8,128)S(1)} %pad_maximum_fusion), channel_id=1, source_target_pairs={{2,0},{4,2},{6,4},{8,6},{10,8},{12,10},{14,12},{16,14},{18,16},{20... | collective-permute-start | bytes 1572872 | tf_op jit(solution)/shard_map/ppermute | solution.py:12
  37.3 11.4 %collective-permute-start.1 = (bf16[2,512,128]{2,1,0:T(8,128)(2,1)S(1)}, bf16[2,512,128]{2,1,0:T(8,128)(2,1)S(1)}, u32[]{:S(2)}, u32[]{:S(2)}) collective-permute-start(bf16[2,512,128]{2,1,0:T(8,128)(2,1)S(1)} %collective-permute-done), channel_id=1, source_target_pairs={{2,0},{4,2},{6,4},{8,6},{10,8},{12,10},{14,12},{16,14},{18,16},{20... | collective-permute-start | bytes 786440 | tf_op jit(solution)/shard_map/ppermute | solution.py:12
  49.4 8.8 %collective-permute-start.2 = (bf16[2,512,128]{2,1,0:T(8,128)(2,1)S(1)}, bf16[2,512,128]{2,1,0:T(8,128)(2,1)S(1)}, u32[]{:S(2)}, u32[]{:S(2)}) collective-permute-start(bf16[2,512,128]{2,1,0:T(8,128)(2,1)S(1)} %collective-permute-done.1), channel_id=1, source_target_pairs={{2,0},{4,2},{6,4},{8,6},{10,8},{12,10},{14,12},{16,14},{18,16},{20... | collective-permute-start | bytes 786440 | tf_op jit(solution)/shard_map/ppermute | solution.py:12
  53.5 21.1 %collective-permute-start.8 = (f32[2,512,128]{2,1,0:T(8,128)S(1)}, f32[2,512,128]{2,1,0:T(8,128)S(1)}, u32[]{:S(2)}, u32[]{:S(2)}) collective-permute-start(f32[2,512,128]{2,1,0:T(8,128)S(1)} %maximum_add_fusion), channel_id=1, source_target_pairs={{2,0},{4,2},{6,4},{8,6},{10,8},{12,10},{14,12},{16,14},{18,16},{20... | collective-permute-start | bytes 1572872 | tf_op jit(solution)/shard_map/ppermute | solution.py:12
  61.5 5.8 %collective-permute-start.3 = (bf16[2,512,128]{2,1,0:T(8,128)(2,1)S(1)}, bf16[2,512,128]{2,1,0:T(8,128)(2,1)S(1)}, u32[]{:S(2)}, u32[]{:S(2)}) collective-permute-start(bf16[2,512,128]{2,1,0:T(8,128)(2,1)S(1)} %collective-permute-done.2), channel_id=1, source_target_pairs={{2,0},{4,2},{6,4},{8,6},{10,8},{12,10},{14,12},{16,14},{18,16},{20... | collective-permute-start | bytes 786440 | tf_op jit(solution)/shard_map/ppermute | solution.py:12
  68.1 11.5 %collective-permute-start.4 = (bf16[2,512,128]{2,1,0:T(8,128)(2,1)S(1)}, bf16[2,512,128]{2,1,0:T(8,128)(2,1)S(1)}, u32[]{:S(2)}, u32[]{:S(2)}) collective-permute-start(bf16[2,512,128]{2,1,0:T(8,128)(2,1)S(1)} %collective-permute-done.3), channel_id=1, source_target_pairs={{2,0},{4,2},{6,4},{8,6},{10,8},{12,10},{14,12},{16,14},{18,16},{20... | collective-permute-start | bytes 786440 | tf_op jit(solution)/shard_map/ppermute | solution.py:12
  72.9 1.7 %copy-start.1 = (bf16[4,512,512]{1,2,0:T(8,128)(2,1)}, bf16[4,512,512]{1,2,0:T(8,128)(2,1)S(1)}, u32[]{:S(2)}) copy-start(bf16[4,512,512]{1,2,0:T(8,128)(2,1)S(1)} %fusion.13) | copy-start | bytes 6291460
  74.7 19.4 %collective-permute-start.9 = (f32[2,512,128]{2,1,0:T(8,128)S(1)}, f32[2,512,128]{2,1,0:T(8,128)S(1)}, u32[]{:S(2)}, u32[]{:S(2)}) collective-permute-start(f32[2,512,128]{2,1,0:T(8,128)S(1)} %maximum_add_fusion.1), channel_id=1, source_target_pairs={{2,0},{4,2},{6,4},{8,6},{10,8},{12,10},{14,12},{16,14},{18,16},{20... | collective-permute-start | bytes 1572872 | tf_op jit(solution)/shard_map/ppermute | solution.py:12
  82.8 11.2 %copy-start.2 = (bf16[4,512,512]{1,2,0:T(8,128)(2,1)}, bf16[4,512,512]{1,2,0:T(8,128)(2,1)S(1)}, u32[]{:S(2)}) copy-start(bf16[4,512,512]{1,2,0:T(8,128)(2,1)S(1)} %fusion.9) | copy-start | bytes 6291460
  82.8 5.8 %collective-permute-start.5 = (bf16[2,512,128]{2,1,0:T(8,128)(2,1)S(1)}, bf16[2,512,128]{2,1,0:T(8,128)(2,1)S(1)}, u32[]{:S(2)}, u32[]{:S(2)}) collective-permute-start(bf16[2,512,128]{2,1,0:T(8,128)(2,1)S(1)} %collective-permute-done.4), channel_id=1, source_target_pairs={{2,0},{4,2},{6,4},{8,6},{10,8},{12,10},{14,12},{16,14},{18,16},{20... | collective-permute-start | bytes 786440 | tf_op jit(solution)/shard_map/ppermute | solution.py:12
  89.4 17.2 %collective-permute-start.6 = (bf16[2,512,128]{2,1,0:T(8,128)(2,1)S(1)}, bf16[2,512,128]{2,1,0:T(8,128)(2,1)S(1)}, u32[]{:S(2)}, u32[]{:S(2)}) collective-permute-start(bf16[2,512,128]{2,1,0:T(8,128)(2,1)S(1)} %collective-permute-done.5), channel_id=1, source_target_pairs={{2,0},{4,2},{6,4},{8,6},{10,8},{12,10},{14,12},{16,14},{18,16},{20... | collective-permute-start | bytes 786440 | tf_op jit(solution)/shard_map/ppermute | solution.py:12
  94.0 5.7 %copy-start.4 = (bf16[4,512,512]{1,2,0:T(8,128)(2,1)}, bf16[4,512,512]{1,2,0:T(8,128)(2,1)S(1)}, u32[]{:S(2)}) copy-start(bf16[4,512,512]{1,2,0:T(8,128)(2,1)S(1)} %fusion.5) | copy-start | bytes 6291460
  94.1 8.7 %collective-permute-start.10 = (f32[2,512,128]{2,1,0:T(8,128)S(1)}, f32[2,512,128]{2,1,0:T(8,128)S(1)}, u32[]{:S(2)}, u32[]{:S(2)}) collective-permute-start(f32[2,512,128]{2,1,0:T(8,128)S(1)} %maximum_add_fusion.2), channel_id=1, source_target_pairs={{2,0},{4,2},{6,4},{8,6},{10,8},{12,10},{14,12},{16,14},{18,16},{20... | collective-permute-start | bytes 1572872 | tf_op jit(solution)/shard_map/ppermute | solution.py:12
  102.8 8.7 %collective-permute-start.11 = (f32[2,512,128]{2,1,0:T(8,128)S(1)}, f32[2,512,128]{2,1,0:T(8,128)S(1)}, u32[]{:S(2)}, u32[]{:S(2)}) collective-permute-start(f32[2,512,128]{2,1,0:T(8,128)S(1)} %maximum_add_fusion.3), channel_id=1, source_target_pairs={{2,0},{4,2},{6,4},{8,6},{10,8},{12,10},{14,12},{16,14},{18,16},{20... | collective-permute-start | bytes 1572872 | tf_op jit(solution)/shard_map/ppermute | solution.py:12
  109.0 10.7 %copy-start.6 = (bf16[4,512,512]{1,2,0:T(8,128)(2,1)}, bf16[4,512,512]{1,2,0:T(8,128)(2,1)S(1)}, u32[]{:S(2)}) copy-start(bf16[4,512,512]{1,2,0:T(8,128)(2,1)S(1)} %fusion.1) | copy-start | bytes 6291460
  111.5 8.7 %collective-permute-start.12 = (f32[2,512,128]{2,1,0:T(8,128)S(1)}, f32[2,512,128]{2,1,0:T(8,128)S(1)}, u32[]{:S(2)}, u32[]{:S(2)}) collective-permute-start(f32[2,512,128]{2,1,0:T(8,128)S(1)} %maximum_add_fusion.4), channel_id=1, source_target_pairs={{2,0},{4,2},{6,4},{8,6},{10,8},{12,10},{14,12},{16,14},{18,16},{20... | collective-permute-start | bytes 1572872 | tf_op jit(solution)/shard_map/ppermute | solution.py:12
  120.3 11.0 %collective-permute-start.13 = (f32[2,512,128]{2,1,0:T(8,128)S(1)}, f32[2,512,128]{2,1,0:T(8,128)S(1)}, u32[]{:S(2)}, u32[]{:S(2)}) collective-permute-start(f32[2,512,128]{2,1,0:T(8,128)S(1)} %maximum_add_fusion.5), channel_id=1, source_target_pairs={{2,0},{4,2},{6,4},{8,6},{10,8},{12,10},{14,12},{16,14},{18,16},{20... | collective-permute-start | bytes 1572872 | tf_op jit(solution)/shard_map/ppermute | solution.py:12
  132.2 2.2 %copy-start.3 = (bf16[4,512,512]{1,2,0:T(8,128)(2,1)S(1)}, bf16[4,512,512]{1,2,0:T(8,128)(2,1)}, u32[]{:S(2)}) copy-start(bf16[4,512,512]{1,2,0:T(8,128)(2,1)} %copy-done.2) | copy-start | bytes 6291460
  132.2 2.8 %copy-start.5 = (bf16[4,512,512]{1,2,0:T(8,128)(2,1)S(1)}, bf16[4,512,512]{1,2,0:T(8,128)(2,1)}, u32[]{:S(2)}) copy-start(bf16[4,512,512]{1,2,0:T(8,128)(2,1)} %copy-done.4) | copy-start | bytes 6291460
  134.4 1.7 %copy-start.7 = (bf16[4,512,512]{1,2,0:T(8,128)(2,1)S(1)}, bf16[4,512,512]{1,2,0:T(8,128)(2,1)}, u32[]{:S(2)}) copy-start(bf16[4,512,512]{1,2,0:T(8,128)(2,1)} %copy-done.6) | copy-start | bytes 6291460
Sparse Core Ops, SparseCore 0:
  132.3 24.9 reduce-scatter.1
where the time goes:
time: 167 us; the launch traced here: 166 us
  starting transfers between devices  47.7 us (29%)
  waiting for transfers between devices  43.7 us (26%)
  matrix products  37.4 us (22%)
  between operations  24.7 us (15%)
  other arithmetic  7.03 us (4%)
  local copies, waits for them, and re-layouts  5.16 us (3%)
    ppermute x14, starting transfers between devices, from_behind(): return lax.ppermute(block, axis, route)  47.7 us
    ppermute x14, waiting for transfers between devices, from_behind(): return lax.ppermute(block, axis, route)  24 us
    reduce_scatter x1, waiting for transfers between devices, shards(): summed = lax.psum_scatter(carried, 'head', scatter_dimension=1, tiled=True)  19.6 us
    dot_general x8, matrix products, block_terms(): jnp.einsum('shd,td->hst', grad_heads, value_block, preferred_element_type...  13.1 us
    dot_general x8, matrix products, block_terms(): jnp.einsum('hst,shd->td', weights_low, grad_heads, preferred_element_type...  7.48 us
    dot_general x8, matrix products, block_terms(): jnp.einsum('shd,td->hst', query_heads, key_block, preferred_element_type=...  5.65 us
    dot_general x8, matrix products, block_terms(): jnp.einsum('hst,shd->td', grad_scores, query_heads, preferred_element_typ...  5.64 us
    dot_general x8, matrix products, block_terms(): jnp.einsum('hst,td->shd', grad_scores, key_block, preferred_element_type=...  5.5 us
  transfers between devices with their start and end apart: 15, of which 8 were waited for; matrix products, arithmetic and copies ran while one was open for 25% of the time, Pallas kernels for 0%

commit v1 on v0

v1 whole, which is shorter than its diff:
```python
import functools

import jax
import jax.numpy as jnp
from jax import lax
from jax.experimental import pallas as pl
from jax.experimental.pallas import tpu as pltpu
from jax.sharding import PartitionSpec as P

LOG2E = 1.4426950408889634
VMEM_LIMIT = 24 << 20
NT = (((1,), (1,)), ((), ()))
NN = (((1,), (0,)), ((), ()))


def dot(a, b, dims):
    return lax.dot_general(a, b, dims, preferred_element_type=jnp.float32)


def terms_kernel(plan, backs, heads, starts_dq, *refs):
    refs = iter(refs)
    stripe = next(refs)
    me = lax.axis_index("seq")
    side = lax.axis_index("head")
    odd = lax.rem(me, 2)
    n = stripe.shape[0]
    flip = me + 1 - 2 * odd
    stripes = (stripe[me], stripe[flip])
    sources = [stripe[lax.rem(me - (1 - odd) * even - odd * uneven + n, n)] for even, uneven in backs]
    kv_refs = [[next(refs)] if whole else [next(refs), next(refs)] for whole, _ in plan]
    groups = sorted({g for _, gs in plan for g in gs})
    query, grad, level = ({g: next(refs) for g in groups} for _ in range(3))
    makes_delta = plan == ((True, (0,)),)
    if makes_delta:
        output = next(refs)
        delta = None
    else:
        delta = {g: next(refs) for g in groups}
    dq_in = {g: next(refs) for g in groups if not starts_dq[g]}
    dq = {g: next(refs) for g in groups}
    send, keep = next(refs), next(refs)
    if makes_delta:
        rows_out = next(refs)
    keys, values, keys_t, dk, dv = refs
    rows, d = keys.shape[1:]
    half = rows // 2
    mine = pl.multiple_of(side * half, half)
    theirs = pl.multiple_of((1 - side) * half, half)
    for b, (whole, _) in enumerate(plan):
        if whole:
            keys[b] = kv_refs[b][0][0]
            values[b] = kv_refs[b][0][1]
        else:
            for ref, at in zip(kv_refs[b], (mine, theirs)):
                keys[b, pl.ds(at, half), :] = ref[0]
                values[b, pl.ds(at, half), :] = ref[1]
        keys_t[b] = keys[b].T
    factor = d**-0.5
    dk[...] = jnp.zeros_like(dk)
    dv[...] = jnp.zeros_like(dv)
    ahead = lax.broadcasted_iota(jnp.int32, (half, half), 0) - lax.broadcasted_iota(
        jnp.int32, (half, half), 1
    )

    def step(h, _):
        cols = pl.ds(pl.multiple_of(h * d, d), d)
        for g in groups:
            source = dq_in.get(g)
            for b, (_, gs) in enumerate(plan):
                if g not in gs:
                    continue
                opened = (sources[b] <= stripes[g]).astype(jnp.int32)
                q = query[g][:, cols]
                do = grad[g][:, cols]
                lse = level[g][pl.ds(h, 1), :] * LOG2E
                if makes_delta:
                    product = do.astype(jnp.float32) * output[:, cols].astype(jnp.float32)
                    high = product.astype(jnp.bfloat16)
                    low = (product - high.astype(jnp.float32)).astype(jnp.bfloat16)
                    ones = jnp.ones((8, d), jnp.bfloat16)
                    dl = (dot(ones, high, NT) + dot(ones, low, NT))[:1]
                    rows_out[0, pl.ds(h, 1), :] = level[g][pl.ds(h, 1), :]
                    rows_out[1, pl.ds(h, 1), :] = dl
                else:
                    dl = delta[g][pl.ds(h, 1), :]
                for t in range(2):
                    a = t * half
                    k = keys[b, a : a + half, :]
                    v = values[b, a : a + half, :]
                    scores = dot(k, q[a:], NT)
                    probs = jnp.exp2(scores * (factor * LOG2E) - lse[:, a:])
                    edge = jnp.where(ahead < opened, probs[:, :half], 0.0)
                    probs = edge if t else jnp.concatenate([edge, probs[:, half:]], axis=1)
                    grad_probs = dot(v, do[a:], NT)
                    grad_scores = (probs * (grad_probs - dl[:, a:])).astype(jnp.bfloat16)
                    dv[b, a : a + half, :] += dot(probs.astype(jnp.bfloat16), do[a:], NN)
                    dk[b, a : a + half, :] += dot(grad_scores, q[a:], NN)
                    part = dot(keys_t[b, :, a : a + half], grad_scores, NN)
                    if source is not None:
                        part = source[cols, a:] + part
                    dq[g][cols, a:] = part
                    source = dq[g]
        return 0

    lax.fori_loop(0, heads, step, 0)
    for b in range(len(plan)):
        keep[b, 0] = dk[b, pl.ds(mine, half), :] * factor
        keep[b, 1] = dv[b, pl.ds(mine, half), :]
        send[b, 0] = (dk[b, pl.ds(theirs, half), :] * factor).astype(jnp.bfloat16)
        send[b, 1] = dv[b, pl.ds(theirs, half), :].astype(jnp.bfloat16)


def terms(plan, backs, kvs, stripe, query, grad, level, delta, dq_in, output=None):
    groups = sorted({g for _, gs in plan for g in gs})
    n = len(plan)
    rows, width = query[0].shape
    d = kvs[0].shape[-1]
    heads = width // d
    starts_dq = [x is None for x in dq_in]
    carried = [dq_in[g] for g in groups if dq_in[g] is not None]
    operands = [stripe, *kvs]
    for per_group in (query, grad, level):
        operands += [per_group[g] for g in groups]
    operands += [output] if output is not None else [delta[g] for g in groups]
    at = len(operands)
    operands += carried
    aliases = {}
    for place, g in enumerate(groups):
        if dq_in[g] is not None:
            aliases[at + len(aliases)] = place
    pairs = sum(len(gs) for _, gs in plan)
    vmem = pl.BlockSpec(memory_space=pltpu.VMEM)
    halves = (n, 2, rows // 2, d)
    extra = [] if output is None else [jax.ShapeDtypeStruct((2, heads, rows), jnp.float32)]
    out = pl.pallas_call(
        functools.partial(terms_kernel, plan, backs, heads, starts_dq),
        out_shape=[jax.ShapeDtypeStruct((width, rows), jnp.float32) for _ in groups]
        + [jax.ShapeDtypeStruct(halves, jnp.bfloat16), jax.ShapeDtypeStruct(halves, jnp.float32)]
        + extra,
        in_specs=[pl.BlockSpec(memory_space=pltpu.SMEM)] + [vmem] * (len(operands) - 1),
        out_specs=[vmem] * (len(groups) + 2 + len(extra)),
        input_output_aliases=aliases,
        scratch_shapes=[
            pltpu.VMEM((n, rows, d), jnp.bfloat16),
            pltpu.VMEM((n, rows, d), jnp.bfloat16),
            pltpu.VMEM((n, d, rows), jnp.bfloat16),
            pltpu.VMEM((n, rows, d), jnp.float32),
            pltpu.VMEM((n, rows, d), jnp.float32),
        ],
        cost_estimate=pl.CostEstimate(
            flops=pairs * heads * rows * rows * d * 8,
            bytes_accessed=4 * rows * width * 2,
            transcendentals=pairs * heads * rows * rows,
        ),
        compiler_params=pltpu.CompilerParams(vmem_limit_bytes=VMEM_LIMIT),
        name="window_terms",
    )(*operands)
    dq = list(dq_in)
    for place, g in enumerate(groups):
        dq[g] = out[place]
    return dq, *out[len(groups) :]


def shards(query, key_rows, value_rows, output, grad_output, log_norm, stripe):
    rows, width = query.shape
    d = key_rows.shape[1]
    heads = width // d
    half = rows // 2
    n = lax.axis_size("seq")
    me = lax.axis_index("seq")
    side = lax.axis_index("head")
    def shift(x, by, only_odd=False):
        route = [(i, (i + by) % n) for i in range(n) if i % 2 or not only_odd]
        return lax.ppermute(x, "seq", route)

    def flip_core(x):
        return lax.ppermute(x, "seq", [(i, i ^ 1) for i in range(n)])

    def flip_head(x):
        return lax.ppermute(x, "head", [(0, 1), (1, 0)])

    kv = jnp.stack([key_rows, value_rows])
    kv_mine = lax.dynamic_slice_in_dim(kv, side * half, half, 1)
    kv_theirs = lax.dynamic_slice_in_dim(kv, (1 - side) * half, half, 1)
    near = [shift(kv_mine, 2), shift(kv_mine, 4)]
    far = [shift(kv_mine, 6), shift(kv_mine, 8, only_odd=True)]

    queries = [query, flip_core(query)]
    grads = [grad_output, flip_core(grad_output)]
    dq, own_send, own_keep, level_delta = terms(
        ((True, (0,)),),
        ((0, 0),),
        [kv],
        stripe,
        queries,
        grads,
        [log_norm],
        None,
        [None, None],
        output,
    )
    other_rows = flip_core(level_delta)
    args = (
        queries,
        grads,
        [log_norm, other_rows[0]],
        [level_delta[1], other_rows[1]],
    )

    near_flip = flip_head(jnp.stack(near))
    far_flip = flip_head(jnp.stack(far))

    dq, near_send, near_keep = terms(
        ((False, (0, 1)), (False, (0, 1))),
        ((2, 2), (4, 4)),
        [near[0], near_flip[0], near[1], near_flip[1]],
        stripe,
        *args,
        dq,
    )
    is_odd = me % 2 == 1
    last = [jnp.where(is_odd, far[1], kv_mine), jnp.where(is_odd, far_flip[1], kv_theirs)]
    dq, far_send, far_keep = terms(
        ((False, (0, 1)), (False, (1,))),
        ((6, 6), (0, 8)),
        [far[0], far_flip[0], *last],
        stripe,
        *args,
        dq,
    )

    grad_query = (dq[0] + flip_core(dq[1])) * (d**-0.5)
    grad_query = grad_query.T.astype(jnp.bfloat16)

    own = own_keep[0] + flip_head(own_send)[0].astype(jnp.float32)
    near_sum = (near_keep + flip_head(near_send).astype(jnp.float32)).astype(jnp.bfloat16)
    back = [shift(near_sum[0], -2), shift(near_sum[1], -4)]
    far_sum = far_keep + flip_head(far_send).astype(jnp.float32)
    far_low = far_sum.astype(jnp.bfloat16)
    back += [shift(far_low[0], -6), shift(far_low[1], -8, only_odd=True)]
    own = own + jnp.where(is_odd, 0.0, far_sum[1])
    for part in back:
        own = own + part.astype(jnp.float32)
    own = own.astype(jnp.bfloat16)
    return grad_query, own[0], own[1]


def solution(mesh):
    placed = (
        P("seq", "head"),
        P("seq", None),
        P("seq", None),
        P("seq", "head"),
        P("seq", "head"),
        P("head", "seq"),
        P(),
    )
    return jax.shard_map(
        shards,
        mesh=mesh,
        in_specs=placed,
        out_specs=(P("seq", "head"), P(("seq", "head"), None), P(("seq", "head"), None)),
        check_vma=False,
    )
```

time: 167 us -> 78.6 us (0.47)
  matrix products: 37.4 us -> 0 us
  between operations: 24.7 us -> 0.91 us
  starting transfers between devices: 47.7 us -> 24.2 us
  Pallas kernels: 0 us -> 22.6 us
  waiting for transfers between devices: 43.7 us -> 23.5 us
  other arithmetic: 7.03 us -> 3.24 us
    dot_general x40 -> x0, matrix products: 37.4 us -> none  [the longest x8 13.1 us: block_terms(): jnp.einsum('shd,td->hst', grad_heads, value_block, preferred_element_type...]
    ppermute x14 -> x17, starting transfers between devices: 47.7 us -> 24.2 us  [the longest x8 18.1 us: shift(): return lax.ppermute(x, 'seq', route)]
    pallas_call x0 -> x3, Pallas kernels: none -> 22.6 us  [terms(): pl.pallas_call(functools.partial(terms_kernel, plan, backs, heads, starts...]
    reduce_scatter x1 -> x0, waiting for transfers between devices: 19.6 us -> none  [shards(): summed = lax.psum_scatter(carried, 'head', scatter_dimension=1, tiled=True)]
    reduce_sum x2 -> x0, other arithmetic: 2.09 us -> none  [the longest x1 1.47 us: stripe_at(): return jnp.sum(jnp.where(slot_ids == where_index, stripe, 0))]
    convert_element_type x2 -> x0, local copies, waits for them, and re-layouts: 2.03 us -> none  [the longest x1 1.37 us: shards(): output_heads.astype(jnp.float32)]
    ppermute x14 -> x17, waiting for transfers between devices: 24 us -> 23.5 us  [the longest x5 11.4 us: flip_head(): return lax.ppermute(x, 'head', [(0, 1), (1, 0)])]
  transfers between devices with their start and end apart: 15 -> 17, of which waited for: 8 -> 7; matrix products, arithmetic and copies ran while one was open for 25% -> 3% of each run, Pallas kernels for 0% -> 29%
where the time goes in v1:
time: 78.6 us; the launch traced here: 78.3 us
  starting transfers between devices  24.2 us (31%)
  waiting for transfers between devices  23.5 us (30%)
  Pallas kernels  22.6 us (29%)
  local copies, waits for them, and re-layouts  3.84 us (5%)
  other arithmetic  3.24 us (4%)
  between operations  0.91 us (1%)
    pallas_call x3, Pallas kernels, terms(): pl.pallas_call(functools.partial(terms_kernel, plan, backs, heads, starts...  22.6 us
    ppermute x8, starting transfers between devices, shift(): return lax.ppermute(x, 'seq', route)  18.1 us
    ppermute x5, waiting for transfers between devices, flip_head(): return lax.ppermute(x, 'head', [(0, 1), (1, 0)])  11.4 us
    ppermute x8, waiting for transfers between devices, shift(): return lax.ppermute(x, 'seq', route)  11 us
    ppermute x5, starting transfers between devices, flip_head(): return lax.ppermute(x, 'head', [(0, 1), (1, 0)])  4.47 us
    unnamed x19, local copies, waits for them, and re-layouts  3.11 us
    another operation x2, other arithmetic, shards(): kv = jnp.stack([key_rows, value_rows])  2.59 us
    ppermute x4, starting transfers between devices, flip_core(): return lax.ppermute(x, 'seq', [(i, i ^ 1) for i in range(n)])  1.66 us
  transfers between devices with their start and end apart: 17, of which 7 were waited for; matrix products, arithmetic and copies ran while one was open for 3% of the time, Pallas kernels for 29%

profile of v1, /device:TPU:1, one launch (start us, length us, event | category | flops | bytes accessed | tf_op | source)
XLA Modules:
  0.0 78.3 jit_solution(3594583147228934347)
XLA Ops:
  0.6 0.0 copy-start
  0.6 1.6 %fusion.8 = bf16[2,256,128]{2,1,0:T(8,128)(2,1)} fusion(s32[]{:T(128)S(6)} %select_n.34, bf16[1,512,128]{2,1,0:T(8,128)(2,1)} %bitcast.51, bf16[1,512,128]{2,1,0:T(8,128)(2,1)} %bitcast.55), kind=kLoop, calls=%fused_computation.19 | loop fusion | flops 262144 | bytes 393220 | tf_op jit(solution)/shard_map/stack | solution.py:182
  2.2 0.0 copy-start.5
  2.2 0.0 copy-start.6
  2.2 2.1 %collective-permute-start.7 = (bf16[2,256,128]{2,1,0:T(8,128)(2,1)}, bf16[2,256,128]{2,1,0:T(8,128)(2,1)S(1)}, u32[]{:S(2)}, u32[]{:S(2)}) collective-permute-start(bf16[2,256,128]{2,1,0:T(8,128)(2,1)} %fusion.8), channel_id=1, source_target_pairs={{0,8},{2,10},{4,12},{6,14},{8,16},{10,18},{12,20},{14,22},{16,24},... | collective-permute-start | bytes 393224 | tf_op jit(solution)/shard_map/ppermute | solution.py:174
  4.4 1.2 %collective-permute-start.6 = (bf16[2,256,128]{2,1,0:T(8,128)(2,1)}, bf16[2,256,128]{2,1,0:T(8,128)(2,1)S(1)}, u32[]{:S(2)}, u32[]{:S(2)}) collective-permute-start(bf16[2,256,128]{2,1,0:T(8,128)(2,1)} %fusion.8), channel_id=1, source_target_pairs={{0,4},{2,6},{4,8},{6,10},{8,12},{10,14},{12,16},{14,18},{16,20},{1... | collective-permute-start | bytes 393224 | tf_op jit(solution)/shard_map/ppermute | solution.py:174
  5.6 2.3 %collective-permute-start = (bf16[2,256,128]{2,1,0:T(8,128)(2,1)}, bf16[2,256,128]{2,1,0:T(8,128)(2,1)S(1)}, u32[]{:S(2)}, u32[]{:S(2)}) collective-permute-start(bf16[2,256,128]{2,1,0:T(8,128)(2,1)} %fusion.8), channel_id=1, source_target_pairs={{0,12},{2,14},{4,16},{6,18},{8,20},{10,22},{12,24},{14,26},{16,28}... | collective-permute-start | bytes 393224 | tf_op jit(solution)/shard_map/ppermute | solution.py:174
  7.9 1.5 %collective-permute-start.3 = (bf16[512,512]{1,0:T(8,128)(2,1)}, bf16[512,512]{1,0:T(8,128)(2,1)S(1)}, u32[]{:S(2)}, u32[]{:S(2)}) collective-permute-start(bf16[512,512]{1,0:T(8,128)(2,1)} %refs_5_.5), channel_id=1, source_target_pairs={{0,2},{2,0},{4,6},{6,4},{8,10},{10,8},{12,14},{14,12},{16,18},{18,... | collective-permute-start | bytes 1572872 | tf_op jit(solution)/shard_map/ppermute | solution.py:177
  9.4 1.0 %pad_maximum_fusion.refs_1_ = bf16[2,512,128]{2,1,0:T(8,128)(2,1)S(1)} fusion(bf16[1,512,128]{2,1,0:T(8,128)(2,1)} %bitcast.56, bf16[1,512,128]{2,1,0:T(8,128)(2,1)} %bitcast.52), kind=kLoop, calls=%fused_computation.6 | loop fusion | flops 131072 | bytes 524288 | tf_op jit(solution)/shard_map/stack | solution.py:182
  10.4 0.0 copy-done
  10.4 0.0 copy-done.5
  10.4 0.0 copy-done.6
  10.4 0.0 copy-start.1
  10.4 1.0 %copy-done.1 = bf16[512,512]{1,0:T(8,128)(2,1)S(1)} copy-done((bf16[512,512]{1,0:T(8,128)(2,1)S(1)}, bf16[512,512]{1,0:T(8,128)(2,1)}, u32[]{:S(2)}) %copy-start.1) | copy-done | bytes 524312
  11.4 0.0 copy-start.3
  11.4 1.0 %copy-done.3 = bf16[512,512]{1,0:T(8,128)(2,1)S(1)} copy-done((bf16[512,512]{1,0:T(8,128)(2,1)S(1)}, bf16[512,512]{1,0:T(8,128)(2,1)}, u32[]{:S(2)}) %copy-start.3) | copy-done | bytes 524312
  12.5 0.0 copy-start.4
  12.5 4.1 %window_terms.3 = (f32[512,512]{1,0:T(8,128)S(1)}, bf16[1,2,256,128]{3,2,1,0:T(8,128)(2,1)S(1)}, f32[1,2,256,128]{3,2,1,0:T(8,128)S(1)}, f32[2,4,512]{2,1,0:T(4,128)S(1)}) custom-call(s32[16]{0:T(128)S(1)} %copy-done.6, bf16[2,512,128]{2,1,0:T(8,128)(2,1)S(1)} %pad_maximum_fusion.refs_1_, bf16[512,512]{1,0:T(8,128)(2,1)S(1)} %copy-done.1, ...), custom_call_target="tpu_custom_call" | custom-call | flops 1073741824 | bytes 2097152 | tf_op jit(solution)/shard_map/window_terms/pallas_call | solution.py:135
  16.6 0.1 collective-permute-start.5
  16.7 1.1 %collective-permute-done.5 = f32[2,4,512]{2,1,0:T(4,128)S(1)} collective-permute-done((f32[2,4,512]{2,1,0:T(4,128)S(1)}, f32[2,4,512]{2,1,0:T(4,128)S(1)}, u32[]{:S(2)}, u32[]{:S(2)}) %collective-permute-start.5) | collective-permute-done | bytes 16416 | tf_op jit(solution)/shard_map/ppermute | solution.py:177
  17.8 2.9 %collective-permute-start.1 = (bf16[2,256,128]{2,1,0:T(8,128)(2,1)}, bf16[2,256,128]{2,1,0:T(8,128)(2,1)S(1)}, u32[]{:S(2)}, u32[]{:S(2)}) collective-permute-start(bf16[2,256,128]{2,1,0:T(8,128)(2,1)} %fusion.8), channel_id=1, source_target_pairs={{2,18},{6,22},{10,26},{14,30},{18,2},{22,6},{26,10},{30,14},{3,19}... | collective-permute-start | bytes 393224 | tf_op jit(solution)/shard_map/ppermute | solution.py:174
  20.7 0.0 collective-permute-done.refs_1_
  20.7 0.0 copy-done.4
  20.7 0.1 collective-permute-start.4
  20.8 4.9 %collective-permute-done.1 = bf16[2,256,128]{2,1,0:T(8,128)(2,1)S(1)} collective-permute-done((bf16[2,256,128]{2,1,0:T(8,128)(2,1)}, bf16[2,256,128]{2,1,0:T(8,128)(2,1)S(1)}, u32[]{:S(2)}, u32[]{:S(2)}) %collective-permute-start.1) | collective-permute-done | bytes 131104 | tf_op jit(solution)/shard_map/ppermute | solution.py:174
  25.7 1.3 %collective-permute-start.10 = (bf16[1,2,256,128]{3,2,1,0:T(8,128)(2,1)S(1)}, bf16[1,2,256,128]{3,2,1,0:T(8,128)(2,1)S(1)}, u32[]{:S(2)}, u32[]{:S(2)}) collective-permute-start(bf16[1,2,256,128]{3,2,1,0:T(8,128)(2,1)S(1)} %get-tuple-element.22), channel_id=1, source_target_pairs={{0,1},{1,0},{2,3},{3,2},{4,5},{5,4},{6,7},{7,6},{8,9},{9,8},{10,11... | collective-permute-start | bytes 393224 | tf_op jit(solution)/shard_map/ppermute | solution.py:180
  27.0 0.0 collective-permute-done.7.refs_3_
  27.0 0.3 collective-permute-start.2
  27.3 0.0 collective-permute-done.6.refs_1_
  27.3 0.0 copy-start.7
  27.3 0.0 copy-start.8
  27.3 1.3 %collective-permute-start.8 = (bf16[2,2,256,128]{3,2,1,0:T(8,128)(2,1)S(1)}, bf16[2,2,256,128]{3,2,1,0:T(8,128)(2,1)S(1)}, u32[]{:S(2)}, u32[]{:S(2)}) collective-permute-start(bf16[2,2,256,128]{3,2,1,0:T(8,128)(2,1)S(1)} %pad_maximum_fusion.2), channel_id=1, source_target_pairs={{0,1},{1,0},{2,3},{3,2},{4,5},{5,4},{6,7},{7,6},{8,9},{9,8},{10,11... | collective-permute-start | bytes 786440 | tf_op jit(solution)/shard_map/ppermute | solution.py:180
  28.6 0.0 copy-done.7
  28.6 0.0 copy-done.8
  28.7 7.0 %collective-permute-done.2 = bf16[2,2,256,128]{3,2,1,0:T(8,128)(2,1)S(1)} collective-permute-done((bf16[2,2,256,128]{3,2,1,0:T(8,128)(2,1)S(1)}, bf16[2,2,256,128]{3,2,1,0:T(8,128)(2,1)S(1)}, u32[]{:S(2)}, u32[]{:S(2)}) %collective-permute-start.2) | collective-permute-done | bytes 262176 | tf_op jit(solution)/shard_map/ppermute | solution.py:180
  35.7 0.0 copy-start.2
  35.7 2.7 %collective-permute-done.8 = bf16[2,2,256,128]{3,2,1,0:T(8,128)(2,1)S(1)} collective-permute-done((bf16[2,2,256,128]{3,2,1,0:T(8,128)(2,1)S(1)}, bf16[2,2,256,128]{3,2,1,0:T(8,128)(2,1)S(1)}, u32[]{:S(2)}, u32[]{:S(2)}) %collective-permute-start.8) | collective-permute-done | bytes 262176 | tf_op jit(solution)/shard_map/ppermute | solution.py:180
  38.5 0.0 collective-permute-done.3.refs_6_
  38.5 0.0 collective-permute-done.4.refs_8_
  38.5 0.0 copy-done.2
  38.5 10.3 %window_terms.4 = (f32[512,512]{1,0:T(8,128)S(1)}, f32[512,512]{1,0:T(8,128)S(1)}, bf16[2,2,256,128]{3,2,1,0:T(8,128)(2,1)S(1)}, f32[2,2,256,128]{3,2,1,0:T(8,128)S(1)}) custom-call(s32[16]{0:T(128)S(1)} %copy-done.6, bf16[2,256,128]{2,1,0:T(8,128)(2,1)S(1)} %collective-permute-done.6.refs_1_, ...), custom_call_target="tpu_custom_call", output_to_operand_aliasing={{0}: (13, {})} | custom-call | flops 4294967296 | bytes 2097152 | tf_op jit(solution)/shard_map/window_terms/pallas_call | solution.py:135
  48.8 1.1 %collective-permute-start.12 = (bf16[2,2,256,128]{3,2,1,0:T(8,128)(2,1)S(1)}, bf16[2,2,256,128]{3,2,1,0:T(8,128)(2,1)S(1)}, u32[]{:S(2)}, u32[]{:S(2)}) collective-permute-start(bf16[2,2,256,128]{3,2,1,0:T(8,128)(2,1)S(1)} %get-tuple-element.26), channel_id=1, source_target_pairs={{0,1},{1,0},{2,3},{3,2},{4,5},{5,4},{6,7},{7,6},{8,9},{9,8},{10,11... | collective-permute-start | bytes 786440 | tf_op jit(solution)/shard_map/ppermute | solution.py:180
  49.9 8.2 %window_terms.5 = (f32[512,512]{1,0:T(8,128)S(1)}, f32[512,512]{1,0:T(8,128)S(1)}, bf16[2,2,256,128]{3,2,1,0:T(8,128)(2,1)S(1)}, f32[2,2,256,128]{3,2,1,0:T(8,128)S(1)}) custom-call(s32[16]{0:T(128)S(1)} %copy-done.6, bf16[2,256,128]{2,1,0:T(8,128)(2,1)S(1)} %collective-permute-done.refs_1_, ...), custom_call_target="tpu_custom_call", output_to_operand_aliasing={{0}: (13, {}), {1}: (14, {})} | custom-call | flops 3221225472 | bytes 2097152 | tf_op jit(solution)/shard_map/window_terms/pallas_call | solution.py:135
  58.1 0.5 collective-permute-start.11
  58.6 0.0 collective-permute-start.9
  58.6 0.0 collective-permute-done.12
  58.6 0.1 add_convert_fusion
  58.7 2.1 %collective-permute-start.13 = (bf16[2,256,128]{2,1,0:T(8,128)(2,1)S(1)}, bf16[2,256,128]{2,1,0:T(8,128)(2,1)S(1)}, u32[]{:S(2)}, u32[]{:S(2)}) collective-permute-start(bf16[2,256,128]{2,1,0:T(8,128)(2,1)S(1)} %get-tuple-element.32), channel_id=1, source_target_pairs={{0,28},{2,30},{4,0},{6,2},{8,4},{10,6},{12,8},{14,10},{16,12},{18,... | collective-permute-start | bytes 393224 | tf_op jit(solution)/shard_map/ppermute | solution.py:174
  60.8 1.5 %collective-permute-start.14 = (bf16[2,256,128]{2,1,0:T(8,128)(2,1)S(1)}, bf16[2,256,128]{2,1,0:T(8,128)(2,1)S(1)}, u32[]{:S(2)}, u32[]{:S(2)}) collective-permute-start(bf16[2,256,128]{2,1,0:T(8,128)(2,1)S(1)} %get-tuple-element.33), channel_id=1, source_target_pairs={{0,24},{2,26},{4,28},{6,30},{8,0},{10,2},{12,4},{14,6},{16,8},{18,... | collective-permute-start | bytes 393224 | tf_op jit(solution)/shard_map/ppermute | solution.py:174
  62.3 1.7 %collective-permute-done.11 = bf16[2,2,256,128]{3,2,1,0:T(8,128)(2,1)S(1)} collective-permute-done((bf16[2,2,256,128]{3,2,1,0:T(8,128)(2,1)S(1)}, bf16[2,2,256,128]{3,2,1,0:T(8,128)(2,1)S(1)}, u32[]{:S(2)}, u32[]{:S(2)}) %collective-permute-start.11) | collective-permute-done | bytes 262176 | tf_op jit(solution)/shard_map/ppermute | solution.py:180
  64.0 0.1 fusion.11
  64.1 4.1 %collective-permute-start.15 = (bf16[2,256,128]{2,1,0:T(8,128)(2,1)S(1)}, bf16[2,256,128]{2,1,0:T(8,128)(2,1)S(1)}, u32[]{:S(2)}, u32[]{:S(2)}) collective-permute-start(bf16[2,256,128]{2,1,0:T(8,128)(2,1)S(1)} %get-tuple-element.34), channel_id=1, source_target_pairs={{0,20},{2,22},{4,24},{6,26},{8,28},{10,30},{12,0},{14,2},{16,4},{1... | collective-permute-start | bytes 393224 | tf_op jit(solution)/shard_map/ppermute | solution.py:174
  68.2 0.0 collective-permute-done.10
  68.2 1.9 %collective-permute-start.16 = (bf16[2,256,128]{2,1,0:T(8,128)(2,1)S(1)}, bf16[2,256,128]{2,1,0:T(8,128)(2,1)S(1)}, u32[]{:S(2)}, u32[]{:S(2)}) collective-permute-start(bf16[2,256,128]{2,1,0:T(8,128)(2,1)S(1)} %get-tuple-element.35), channel_id=1, source_target_pairs={{2,18},{6,22},{10,26},{14,30},{18,2},{22,6},{26,10},{30,14},{3,19}... | collective-permute-start | bytes 393224 | tf_op jit(solution)/shard_map/ppermute | solution.py:174
  70.2 0.0 collective-permute-done.13
  70.2 0.0 collective-permute-done.14
  70.2 1.3 %collective-permute-done.15 = bf16[2,256,128]{2,1,0:T(8,128)(2,1)S(1)} collective-permute-done((bf16[2,256,128]{2,1,0:T(8,128)(2,1)S(1)}, bf16[2,256,128]{2,1,0:T(8,128)(2,1)S(1)}, u32[]{:S(2)}, u32[]{:S(2)}) %collective-permute-start.15) | collective-permute-done | bytes 131104 | tf_op jit(solution)/shard_map/ppermute | solution.py:174
  71.5 4.8 %collective-permute-done.16 = bf16[2,256,128]{2,1,0:T(8,128)(2,1)S(1)} collective-permute-done((bf16[2,256,128]{2,1,0:T(8,128)(2,1)S(1)}, bf16[2,256,128]{2,1,0:T(8,128)(2,1)S(1)}, u32[]{:S(2)}, u32[]{:S(2)}) %collective-permute-start.16) | collective-permute-done | bytes 131104 | tf_op jit(solution)/shard_map/ppermute | solution.py:174
  76.3 0.1 fusion.7
  76.4 0.7 slice_bitcast_fusion.8
  77.1 0.0 collective-permute-done.9
  77.1 0.3 fusion
  77.3 1.0 %copy.13 = bf16[512,512]{1,0:T(8,128)(2,1)} copy(bf16[512,512]{0,1:T(8,128)(2,1)S(1)} %fusion) | data formatting | bytes 1048576
  (10 shorter events, 0.2 us)
Async XLA Ops:
  0.6 9.7 %copy-start = (bf16[512,512]{1,0:T(8,128)(2,1)S(1)}, bf16[512,512]{1,0:T(8,128)(2,1)}, u32[]{:S(2)}) copy-start(bf16[512,512]{1,0:T(8,128)(2,1)} %refs_5_.3) | copy-start | bytes 1572868
  2.2 8.1 %copy-start.5 = (f32[4,512]{1,0:T(4,128)S(1)}, f32[4,512]{1,0:T(4,128)}, u32[]{:S(2)}) copy-start(f32[4,512]{1,0:T(4,128)} %refs_9_.3) | copy-start | bytes 24580
  2.2 8.1 %copy-start.6 = (s32[16]{0:T(128)S(1)}, s32[16]{0:T(128)}, u32[]{:S(2)}) copy-start(s32[16]{0:T(128)} %refs_0_.5) | copy-start | bytes 196
  2.2 24.8 %collective-permute-start.7 = (bf16[2,256,128]{2,1,0:T(8,128)(2,1)}, bf16[2,256,128]{2,1,0:T(8,128)(2,1)S(1)}, u32[]{:S(2)}, u32[]{:S(2)}) collective-permute-start(bf16[2,256,128]{2,1,0:T(8,128)(2,1)} %fusion.8), channel_id=1, source_target_pairs={{0,8},{2,10},{4,12},{6,14},{8,16},{10,18},{12,20},{14,22},{16,24},... | collective-permute-start | bytes 393224 | tf_op jit(solution)/shard_map/ppermute | solution.py:174
  4.4 22.9 %collective-permute-start.6 = (bf16[2,256,128]{2,1,0:T(8,128)(2,1)}, bf16[2,256,128]{2,1,0:T(8,128)(2,1)S(1)}, u32[]{:S(2)}, u32[]{:S(2)}) collective-permute-start(bf16[2,256,128]{2,1,0:T(8,128)(2,1)} %fusion.8), channel_id=1, source_target_pairs={{0,4},{2,6},{4,8},{6,10},{8,12},{10,14},{12,16},{14,18},{16,20},{1... | collective-permute-start | bytes 393224 | tf_op jit(solution)/shard_map/ppermute | solution.py:174
  5.6 15.1 %collective-permute-start = (bf16[2,256,128]{2,1,0:T(8,128)(2,1)}, bf16[2,256,128]{2,1,0:T(8,128)(2,1)S(1)}, u32[]{:S(2)}, u32[]{:S(2)}) collective-permute-start(bf16[2,256,128]{2,1,0:T(8,128)(2,1)} %fusion.8), channel_id=1, source_target_pairs={{0,12},{2,14},{4,16},{6,18},{8,20},{10,22},{12,24},{14,26},{16,28}... | collective-permute-start | bytes 393224 | tf_op jit(solution)/shard_map/ppermute | solution.py:174
  7.9 30.6 %collective-permute-start.3 = (bf16[512,512]{1,0:T(8,128)(2,1)}, bf16[512,512]{1,0:T(8,128)(2,1)S(1)}, u32[]{:S(2)}, u32[]{:S(2)}) collective-permute-start(bf16[512,512]{1,0:T(8,128)(2,1)} %refs_5_.5), channel_id=1, source_target_pairs={{0,2},{2,0},{4,6},{6,4},{8,10},{10,8},{12,14},{14,12},{16,18},{18,... | collective-permute-start | bytes 1572872 | tf_op jit(solution)/shard_map/ppermute | solution.py:177
  10.4 1.0 %copy-start.1 = (bf16[512,512]{1,0:T(8,128)(2,1)S(1)}, bf16[512,512]{1,0:T(8,128)(2,1)}, u32[]{:S(2)}) copy-start(bf16[512,512]{1,0:T(8,128)(2,1)} %refs_5_.5) | copy-start | bytes 1572868
  11.4 1.0 %copy-start.3 = (bf16[512,512]{1,0:T(8,128)(2,1)S(1)}, bf16[512,512]{1,0:T(8,128)(2,1)}, u32[]{:S(2)}) copy-start(bf16[512,512]{1,0:T(8,128)(2,1)} %refs_7_.3) | copy-start | bytes 1572868
  12.5 8.2 %copy-start.4 = (bf16[512,512]{1,0:T(8,128)(2,1)S(1)}, bf16[512,512]{1,0:T(8,128)(2,1)}, u32[]{:S(2)}) copy-start(bf16[512,512]{1,0:T(8,128)(2,1)} %refs_7_.3) | copy-start | bytes 1572868
  16.6 1.2 %collective-permute-start.5 = (f32[2,4,512]{2,1,0:T(4,128)S(1)}, f32[2,4,512]{2,1,0:T(4,128)S(1)}, u32[]{:S(2)}, u32[]{:S(2)}) collective-permute-start(f32[2,4,512]{2,1,0:T(4,128)S(1)} %get-tuple-element.15), channel_id=1, source_target_pairs={{0,2},{2,0},{4,6},{6,4},{8,10},{10,8},{12,14},{14,12},{16,18},{18,... | collective-permute-start | bytes 49160 | tf_op jit(solution)/shard_map/ppermute | solution.py:177
  17.8 7.8 %collective-permute-start.1 = (bf16[2,256,128]{2,1,0:T(8,128)(2,1)}, bf16[2,256,128]{2,1,0:T(8,128)(2,1)S(1)}, u32[]{:S(2)}, u32[]{:S(2)}) collective-permute-start(bf16[2,256,128]{2,1,0:T(8,128)(2,1)} %fusion.8), channel_id=1, source_target_pairs={{2,18},{6,22},{10,26},{14,30},{18,2},{22,6},{26,10},{30,14},{3,19}... | collective-permute-start | bytes 393224 | tf_op jit(solution)/shard_map/ppermute | solution.py:174
  20.7 17.8 %collective-permute-start.4 = (bf16[512,512]{1,0:T(8,128)(2,1)S(1)}, bf16[512,512]{1,0:T(8,128)(2,1)S(1)}, u32[]{:S(2)}, u32[]{:S(2)}) collective-permute-start(bf16[512,512]{1,0:T(8,128)(2,1)S(1)} %copy-done.4), channel_id=1, source_target_pairs={{0,2},{2,0},{4,6},{6,4},{8,10},{10,8},{12,14},{14,12},{16,18},{18,... | collective-permute-start | bytes 1572872 | tf_op jit(solution)/shard_map/ppermute | solution.py:177
  25.7 42.6 %collective-permute-start.10 = (bf16[1,2,256,128]{3,2,1,0:T(8,128)(2,1)S(1)}, bf16[1,2,256,128]{3,2,1,0:T(8,128)(2,1)S(1)}, u32[]{:S(2)}, u32[]{:S(2)}) collective-permute-start(bf16[1,2,256,128]{3,2,1,0:T(8,128)(2,1)S(1)} %get-tuple-element.22), channel_id=1, source_target_pairs={{0,1},{1,0},{2,3},{3,2},{4,5},{5,4},{6,7},{7,6},{8,9},{9,8},{10,11... | collective-permute-start | bytes 393224 | tf_op jit(solution)/shard_map/ppermute | solution.py:180
  27.0 8.6 %collective-permute-start.2 = (bf16[2,2,256,128]{3,2,1,0:T(8,128)(2,1)S(1)}, bf16[2,2,256,128]{3,2,1,0:T(8,128)(2,1)S(1)}, u32[]{:S(2)}, u32[]{:S(2)}) collective-permute-start(bf16[2,2,256,128]{3,2,1,0:T(8,128)(2,1)S(1)} %pad_maximum_fusion.1), channel_id=1, source_target_pairs={{0,1},{1,0},{2,3},{3,2},{4,5},{5,4},{6,7},{7,6},{8,9},{9,8},{10,11... | collective-permute-start | bytes 786440 | tf_op jit(solution)/shard_map/ppermute | solution.py:180
  27.3 1.4 %copy-start.7 = (bf16[512,128]{1,0:T(8,128)(2,1)S(1)}, bf16[512,128]{1,0:T(8,128)(2,1)}, u32[]{:S(2)}) copy-start(bf16[512,128]{1,0:T(8,128)(2,1)} %param.8) | copy-start | bytes 393220
  27.3 1.4 %copy-start.8 = (bf16[512,128]{1,0:T(8,128)(2,1)S(1)}, bf16[512,128]{1,0:T(8,128)(2,1)}, u32[]{:S(2)}) copy-start(bf16[512,128]{1,0:T(8,128)(2,1)} %param.9) | copy-start | bytes 393220
  27.3 11.2 %collective-permute-start.8 = (bf16[2,2,256,128]{3,2,1,0:T(8,128)(2,1)S(1)}, bf16[2,2,256,128]{3,2,1,0:T(8,128)(2,1)S(1)}, u32[]{:S(2)}, u32[]{:S(2)}) collective-permute-start(bf16[2,2,256,128]{3,2,1,0:T(8,128)(2,1)S(1)} %pad_maximum_fusion.2), channel_id=1, source_target_pairs={{0,1},{1,0},{2,3},{3,2},{4,5},{5,4},{6,7},{7,6},{8,9},{9,8},{10,11... | collective-permute-start | bytes 786440 | tf_op jit(solution)/shard_map/ppermute | solution.py:180
  35.7 2.8 %copy-start.2 = (bf16[512,512]{1,0:T(8,128)(2,1)S(1)}, bf16[512,512]{1,0:T(8,128)(2,1)}, u32[]{:S(2)}) copy-start(bf16[512,512]{1,0:T(8,128)(2,1)} %refs_5_.5) | copy-start | bytes 1572868
  48.8 9.8 %collective-permute-start.12 = (bf16[2,2,256,128]{3,2,1,0:T(8,128)(2,1)S(1)}, bf16[2,2,256,128]{3,2,1,0:T(8,128)(2,1)S(1)}, u32[]{:S(2)}, u32[]{:S(2)}) collective-permute-start(bf16[2,2,256,128]{3,2,1,0:T(8,128)(2,1)S(1)} %get-tuple-element.26), channel_id=1, source_target_pairs={{0,1},{1,0},{2,3},{3,2},{4,5},{5,4},{6,7},{7,6},{8,9},{9,8},{10,11... | collective-permute-start | bytes 786440 | tf_op jit(solution)/shard_map/ppermute | solution.py:180
  58.1 5.9 %collective-permute-start.11 = (bf16[2,2,256,128]{3,2,1,0:T(8,128)(2,1)S(1)}, bf16[2,2,256,128]{3,2,1,0:T(8,128)(2,1)S(1)}, u32[]{:S(2)}, u32[]{:S(2)}) collective-permute-start(bf16[2,2,256,128]{3,2,1,0:T(8,128)(2,1)S(1)} %get-tuple-element.24), channel_id=1, source_target_pairs={{0,1},{1,0},{2,3},{3,2},{4,5},{5,4},{6,7},{7,6},{8,9},{9,8},{10,11... | collective-permute-start | bytes 786440 | tf_op jit(solution)/shard_map/ppermute | solution.py:180
  58.6 18.5 %collective-permute-start.9 = (f32[512,512]{1,0:T(8,128)S(1)}, f32[512,512]{1,0:T(8,128)S(1)}, u32[]{:S(2)}, u32[]{:S(2)}) collective-permute-start(f32[512,512]{1,0:T(8,128)S(1)} %get-tuple-element.20), channel_id=1, source_target_pairs={{0,2},{2,0},{4,6},{6,4},{8,10},{10,8},{12,14},{14,12},{16,18},{18,... | collective-permute-start | bytes 3145736 | tf_op jit(solution)/shard_map/ppermute | solution.py:177
  58.7 11.4 %collective-permute-start.13 = (bf16[2,256,128]{2,1,0:T(8,128)(2,1)S(1)}, bf16[2,256,128]{2,1,0:T(8,128)(2,1)S(1)}, u32[]{:S(2)}, u32[]{:S(2)}) collective-permute-start(bf16[2,256,128]{2,1,0:T(8,128)(2,1)S(1)} %get-tuple-element.32), channel_id=1, source_target_pairs={{0,28},{2,30},{4,0},{6,2},{8,4},{10,6},{12,8},{14,10},{16,12},{18,... | collective-permute-start | bytes 393224 | tf_op jit(solution)/shard_map/ppermute | solution.py:174
  60.8 9.4 %collective-permute-start.14 = (bf16[2,256,128]{2,1,0:T(8,128)(2,1)S(1)}, bf16[2,256,128]{2,1,0:T(8,128)(2,1)S(1)}, u32[]{:S(2)}, u32[]{:S(2)}) collective-permute-start(bf16[2,256,128]{2,1,0:T(8,128)(2,1)S(1)} %get-tuple-element.33), channel_id=1, source_target_pairs={{0,24},{2,26},{4,28},{6,30},{8,0},{10,2},{12,4},{14,6},{16,8},{18,... | collective-permute-start | bytes 393224 | tf_op jit(solution)/shard_map/ppermute | solution.py:174
  64.1 7.4 %collective-permute-start.15 = (bf16[2,256,128]{2,1,0:T(8,128)(2,1)S(1)}, bf16[2,256,128]{2,1,0:T(8,128)(2,1)S(1)}, u32[]{:S(2)}, u32[]{:S(2)}) collective-permute-start(bf16[2,256,128]{2,1,0:T(8,128)(2,1)S(1)} %get-tuple-element.34), channel_id=1, source_target_pairs={{0,20},{2,22},{4,24},{6,26},{8,28},{10,30},{12,0},{14,2},{16,4},{1... | collective-permute-start | bytes 393224 | tf_op jit(solution)/shard_map/ppermute | solution.py:174
  68.2 8.0 %collective-permute-start.16 = (bf16[2,256,128]{2,1,0:T(8,128)(2,1)S(1)}, bf16[2,256,128]{2,1,0:T(8,128)(2,1)S(1)}, u32[]{:S(2)}, u32[]{:S(2)}) collective-permute-start(bf16[2,256,128]{2,1,0:T(8,128)(2,1)S(1)} %get-tuple-element.35), channel_id=1, source_target_pairs={{2,18},{6,22},{10,26},{14,30},{18,2},{22,6},{26,10},{30,14},{3,19}... | collective-permute-start | bytes 393224 | tf_op jit(solution)/shard_map/ppermute | solution.py:174
